TPU v7x, 128 devices: a whole 4x4x4 slice. The times are simulated.
128 devices in a mesh: cp: 32 (over y, z, core), ep: 4 (over x).
Axes of the slice: x: 4, y: 4, z: 4, core: 2. Of those that a mesh axis runs over, the one named last changes fastest.
Arguments:
- residual: bfloat16 [4096, 6144], P('cp'), may hold values from -90 to 90
- queries: bfloat16 [4096, 3072], P('cp', 'ep'), may hold values from -256 to 256
- key_proj: bfloat16 [4096, 512], P('cp', 'ep'), may hold values from -8 to 8
- value_proj: bfloat16 [4096, 512], P('cp', 'ep'), may hold values from -12 to 12
- out_weight: bfloat16 [3072, 6144], P('ep'), may hold values from -0.109375 to 0.109375
- norm_gain: float32 [6144], replicated, may hold values from 0.1 to 1.9
- doc_ids: int32 [4096], replicated, may hold values from 0 to 11, never falling along the last dimension, each value on 1 to 1024 neighbouring positions
- block_order: int32 [32], replicated, may hold values from 0 to 31, each once
- expert_ids: int32 [4096, 2], P('cp'), may hold values from 0 to 7, as said below
- route_logits: float32 [4096, 2], P('cp'), may hold values from -12 to 12
- gate_weight: bfloat16 [4, 6144, 8192], P('ep', None, 'cp'), may hold values from -0.078125 to 0.078125
- up_weight: bfloat16 [4, 6144, 8192], P('ep', None, 'cp'), may hold values from -0.078125 to 0.078125
- down_weight: bfloat16 [4, 8192, 6144], P('ep', 'cp'), may hold values from -0.0625 to 0.0625
Outputs:
- hidden_state: bfloat16 [4096, 6144], P('cp', 'ep')
- expert_mix: bfloat16 [4096, 6144], P('cp', 'ep')
Inputs may be any that keep to these rules, and one draw needn't show every extreme that they name: `expert_ids`: each row names two different experts; within the 128 rows of one cp index no expert is named by more than 40 rows. `doc_ids`: document numbers never fall along the sequence. `block_order`: each block number appears once.
All inputs are finite; a program needn't handle non-finite values.
Results may differ from a plain program's by a relative error of at most 0.02.
Values may be sent and summed in bfloat16 or wider, within the bound.
No kernel may reach another device: no remote copies, remote signals or barrier semaphores. Data moves between devices by JAX's collectives and lax.ppermute only.
A program may use at most 128 MiB of HBM per device.

v0:
```python
import math
import jax
import jax.numpy as jnp
from jax import lax
from jax.sharding import PartitionSpec as P

HD = 128
CAP = 40
EPS = 1e-05
NEG = -1e30


def in_one_piece(arrays, axis, dim, along):
    both = jnp.concatenate(arrays, axis=along)
    out, at, outs = (lax.all_gather(both, axis, axis=dim, tiled=True), 0, [])
    for a in arrays:
        outs.append(lax.slice_in_dim(out, at, at + a.shape[along], axis=along))
        at += a.shape[along]
    return tuple(outs)


def cut_along(shard, dim, size):
    before, after = (shard.shape[:dim], shard.shape[dim + 1 :])
    return jnp.moveaxis(shard.reshape(*before, size, -1, *after), dim, 0)


def summed_on_arrival(shard, axis, dim):
    blocks = cut_along(shard, dim, lax.axis_size(axis))
    arrived = lax.all_to_all(blocks, axis, split_axis=0, concat_axis=0, tiled=True)
    return arrived.astype(jnp.float32).sum(axis=0)


def expert_hidden(rows_in, gate_weight, up_weight):
    gated = jnp.dot(rows_in, gate_weight[0], preferred_element_type=jnp.float32)
    lifted = jnp.dot(rows_in, up_weight[0], preferred_element_type=jnp.float32)
    return (jax.nn.silu(gated) * lifted).astype(jnp.bfloat16)


def local(
    residual,
    queries,
    key_proj,
    value_proj,
    out_weight,
    norm_gain,
    doc_ids,
    block_order,
    expert_ids,
    route_logits,
    gate_weight,
    up_weight,
    down_weight,
):
    tokens = residual.shape[0]
    kv_heads = key_proj.shape[1] // HD
    group_size = queries.shape[1] // HD // kv_heads
    score_scale = 1.0 / math.sqrt(HD)
    cp_rank = lax.axis_index("cp")
    ep_rank = lax.axis_index("ep")
    ep_count = lax.axis_size("ep")
    placed = lax.dynamic_slice_in_dim(block_order, cp_rank, 1)[0]
    own_pos = placed * tokens + jnp.arange(tokens, dtype=jnp.int32)
    own_docs = lax.dynamic_slice_in_dim(doc_ids, placed * tokens, tokens)
    query_grid = queries.reshape(tokens, kv_heads, group_size, HD)

    def attend_all(running, shard_piece):
        piece_keys, piece_values, piece_docs, piece_pos = shard_piece
        allowed = (piece_docs[None, :] == own_docs[:, None]) & (
            piece_pos[None, :] <= own_pos[:, None]
        )
        piece_width = piece_keys.shape[0]
        running_max, row_total, weighted = running[0]
        query_rows = query_grid[:, 0].reshape(tokens * group_size, HD)
        scores = lax.dot_general(
            query_rows, piece_keys, (((1,), (1,)), ((), ())), preferred_element_type=jnp.float32
        )
        scores = scores.reshape(tokens, group_size, piece_width) * score_scale
        scores = jnp.where(allowed[:, None, :], scores, NEG)
        new_max = jnp.maximum(running_max, jnp.max(scores, axis=2))
        weights = jnp.where(allowed[:, None, :], jnp.exp(scores - new_max[:, :, None]), 0.0)
        row_total = jnp.sum(weights, axis=2)
        value_mix = jnp.dot(
            weights.astype(jnp.bfloat16).reshape(tokens * group_size, piece_width),
            piece_values,
            preferred_element_type=jnp.float32,
        )
        weighted = value_mix.reshape(tokens, group_size, HD)
        updated = [(new_max, row_total, weighted)]
        return tuple(updated)

    start_state = tuple(
        (
            (
                jnp.full((tokens, group_size), NEG, jnp.float32),
                jnp.zeros((tokens, group_size), jnp.float32),
                jnp.zeros((tokens, group_size, HD), jnp.float32),
            )
            for kv_index in range(kv_heads)
        )
    )
    shard_piece = (
        *in_one_piece((key_proj, value_proj), "cp", 0, 1),
        lax.all_gather(own_docs, "cp", axis=0, tiled=True),
        lax.all_gather(own_pos, "cp", axis=0, tiled=True),
    )
    needed = jnp.any(
        (shard_piece[2][None, :] == own_docs[:, None])
        & (shard_piece[3][None, :] <= own_pos[:, None])
    )
    attn_state = lax.cond(
        needed, lambda inner: attend_all(inner, shard_piece), lambda inner: inner, start_state
    )
    attended = jnp.concatenate(
        [
            (weighted / row_total[:, :, None]).reshape(tokens, group_size * HD)
            for running_max, row_total, weighted in attn_state
        ],
        axis=1,
    ).astype(jnp.bfloat16)
    projected = jnp.dot(attended, out_weight, preferred_element_type=jnp.float32)
    quarter_width = residual.shape[1] // ep_count
    summed = lax.psum(projected.astype(jnp.bfloat16), "ep").astype(jnp.float32)
    hidden_full = (residual.astype(jnp.float32) + summed).astype(jnp.bfloat16)
    hidden_state = lax.dynamic_slice_in_dim(hidden_full, ep_rank * quarter_width, quarter_width, 1)
    values_wide = hidden_full.astype(jnp.float32)
    mean_square = jnp.mean(values_wide * values_wide, axis=1, keepdims=True)
    normed = (values_wide * lax.rsqrt(mean_square + EPS) * norm_gain).astype(jnp.bfloat16)
    logit_gap = route_logits[:, 1] - route_logits[:, 0]
    first_share = 1.0 / (1.0 + jnp.exp(logit_gap))
    second_share = 1.0 / (1.0 + jnp.exp(-logit_gap))
    slot_ids = jnp.arange(CAP, dtype=jnp.int32)
    expert = ep_rank * gate_weight.shape[0]
    is_member = ((expert_ids[:, 0] == expert) | (expert_ids[:, 1] == expert)).astype(jnp.int32)
    slot_index = jnp.cumsum(is_member) - is_member
    selector = ((slot_index[None, :] == slot_ids[:, None]) & (is_member[None, :] == 1)).astype(
        jnp.bfloat16
    )
    route_share = jnp.where(expert_ids[:, 0] == expert, first_share, 0.0) + jnp.where(
        expert_ids[:, 1] == expert, second_share, 0.0
    )
    slot_index, selector, route_share = (slot_index, selector, route_share)
    packed = jnp.dot(selector, normed, preferred_element_type=jnp.float32).astype(jnp.bfloat16)
    hidden = expert_hidden(lax.all_gather(packed, "cp", axis=0, tiled=True), gate_weight, up_weight)
    rows_in = lax.slice_in_dim(hidden, 0, CAP * lax.axis_size("cp"), axis=0)
    expert_sum = lax.psum_scatter(
        jnp.dot(rows_in, down_weight[0], preferred_element_type=jnp.float32).astype(jnp.bfloat16),
        "cp",
        scatter_dimension=0,
        tiled=True,
    ).astype(jnp.float32)
    gathered = jnp.take(expert_sum, jnp.minimum(slot_index, CAP - 1), axis=0)
    contribution = gathered * route_share[:, None]
    mixed_share = summed_on_arrival(contribution.astype(jnp.bfloat16), "ep", 1)
    return (hidden_state, mixed_share.astype(jnp.bfloat16))


def solution(mesh):
    return jax.shard_map(
        local,
        mesh=mesh,
        in_specs=(
            P("cp", None),
            P("cp", "ep"),
            P("cp", "ep"),
            P("cp", "ep"),
            P("ep", None),
            P(),
            P(),
            P(),
            P("cp", None),
            P("cp", None),
            P("ep", None, "cp"),
            P("ep", None, "cp"),
            P("ep", "cp", None),
        ),
        out_specs=(P("cp", "ep"), P("cp", "ep")),
        check_vma=False,
    )
```

profile of v0, /device:TPU:0, one launch (start us, length us, event | category | flops | bytes accessed | tf_op | source)
XLA Modules:
  0.0 387.8 jit_solution(3691068288422893904)
XLA Ops:
  7.2 1.6 pad_maximum_fusion
  8.9 1.2 dynamic_slice.9
  10.8 0.8 dynamic_slice.10
  11.5 23.1 %all-gather.1 = s32[32,1,128]{2,1,0:T(1,128)S(1)} all-gather(s32[1,1,128]{2,1,0:T(1,128)S(1)} %fusion.40), channel_id=1, replica_groups=mesh['cp'=32,'ep'=4] {'cp'}, dimensions={0}, use_global_device_ids=true | all-gather | bytes 16896 | tf_op jit(solution)/shard_map/all_gather | solution.py:104
  34.6 0.8 dynamic-slice_bitcast_fusion
  35.4 20.4 %all-gather = s32[32,1,128]{2,1,0:T(1,128)S(1)} all-gather(s32[1,1,128]{2,1,0:T(1,128)S(1)} %dynamic-slice_bitcast_fusion), channel_id=1, replica_groups=mesh['cp'=32,'ep'=4] {'cp'}, dimensions={0}, use_global_device_ids=true | all-gather | bytes 16896 | tf_op jit(solution)/shard_map/all_gather | solution.py:103
  56.4 1.3 and_reduce_fusion
  58.4 15.5 %conditional.1 = (f32[128,6]{0,1:T(8,128)}, f32[128,6,128]{0,2,1:T(8,128)S(1)}) conditional(s32[]{:T(128)} %convert_element_type.64, () %tuple.16, (s32[4096]{0:T(1024)}, s32[128]{0:T(128)}, s32[4096]{0:T(1024)S(1)}, s32[128]{0:T(128)}, bf16[128,768]{1,0:T(8,128)(2,1)}, /*index=5*/bf16[4096,256]{1,0:T(8,128)(2,1)}) %tuple.42), branch_computations={%region_1.0_spmd, %region_2.5_spmd} | conditional | flops 1653079296 | bytes 53465160 | solution.py:110
  58.4 2.0 compare_and_fusion
  60.4 1.1 copy.79
  61.5 3.9 %fusion = (f32[128,6]{0,1:T(8,128)S(1)}, f32[128,6,4096]{2,0,1:T(8,128)S(1)}) fusion(pred[128,4096]{1,0:T(8,128)(4,1)} %compare_and_fusion, bf16[128,6,128]{0,2,1:T(8,128)(2,1)S(1)} %bitcast.58, bf16[4096,256]{1,0:T(8,128)(2,1)} %get-tuple-element.20), kind=kOutput, calls=%fused_computation.3 | convolution fusion | flops 814742784 | bytes 14355456 | tf_op jit(solution)/shard_map/cond/branch_1_fun/dot_general | solution.py:74
  65.5 4.7 %fusion.2 = f32[128,6]{0,1:T(8,128)} fusion(f32[128,6,4096]{2,0,1:T(8,128)S(1)} %get-tuple-element.61, f32[128,6]{0,1:T(8,128)S(1)} %broadcast_maximum_fusion, pred[128,4096]{1,0:T(8,128)(4,1)S(1)} %copy-done.1), kind=kLoop, calls=%fused_computation.5 | loop fusion | flops 15727872 | bytes 13113344 | tf_op jit(solution)/shard_map/cond/branch_1_fun/reduce_sum | solution.py:81
  70.2 3.6 fusion.3
  74.6 6.3 %convolution_convert_fusion.1 = bf16[128,6144]{1,0:T(8,128)(2,1)} fusion(bf16[128,768]{0,1:T(8,128)(2,1)S(1)} %bitcast.57, bf16[768,6144]{1,0:T(8,128)(2,1)} %param.19), kind=kOutput, calls=%fused_computation.19 | convolution fusion | flops 1208745984 | bytes 11206656 | tf_op jit(solution)/shard_map/dot_general | solution.py:120
  81.3 49.7 %all-reduce.2.cloned.1.call-done = bf16[128,6144]{1,0:T(8,128)(2,1)} async-done(((bf16[128,6144]{1,0:T(8,128)(2,1)}), bf16[128,6144]{1,0:T(8,128)(2,1)}) %all-reduce.2.cloned.1.call-update) | async-done | bytes 1572880 | tf_op jit(solution)/shard_map/psum | solution.py:122
  131.0 2.6 fusion.14
  133.6 1.1 copy-done.2
  134.8 1.4 convolution_convert_fusion.2
  136.4 70.2 %all-gather.7.cloned.1.call-done = bf16[1280,6144]{1,0:T(8,128)(2,1)} async-done(((bf16[40,6144]{1,0:T(8,128)(2,1)}), bf16[1280,6144]{1,0:T(8,128)(2,1)}) %all-gather.7.cloned.1.call-update) | async-done | bytes 15728656 | tf_op jit(solution)/shard_map/all_gather | solution.py:143
  206.7 9.4 %fusion.22 = f32[1280,256]{1,0:T(8,128)S(1)} fusion(bf16[1280,6144]{1,0:T(8,128)(2,1)} %all-gather.7.cloned.1.call-done, bf16[1,6144,256]{2,1,0:T(8,128)(2,1)} %param.25), kind=kOutput, calls=%fused_computation.32 | convolution fusion | flops 4026531840 | bytes 20185088 | tf_op jit(solution)/shard_map/dot_general | solution.py:34
  216.1 1.5 copy-done.9
  217.5 0.9 copy-done.10
  218.4 4.6 %fusion.27 = bf16[1280,256]{1,0:T(8,128)(2,1)S(1)} fusion(bf16[1280,6144]{1,0:T(8,128)(2,1)S(1)} %copy-done.9, bf16[1,6144,256]{2,1,0:T(8,128)(2,1)S(1)} %copy-done.10, f32[1280,256]{1,0:T(8,128)S(1)} %fusion.22), kind=kOutput, calls=%fused_computation.36 | convolution fusion | flops 4028497920 | bytes 20840448 | tf_op jit(solution)/shard_map/dot_general | solution.py:35
  223.1 7.8 %convolution_convert_fusion = bf16[1280,6144]{1,0:T(8,128)(2,1)} fusion(bf16[1280,256]{1,0:T(8,128)(2,1)S(1)} %fusion.27, bf16[1,256,6144]{2,1,0:T(8,128)(2,1)S(1)} %copy-done), kind=kOutput, calls=%fused_computation.18 | convolution fusion | flops 4034396160 | bytes 19529728 | tf_op jit(solution)/shard_map/dot_general | solution.py:146
  231.6 111.8 %reduce-scatter.2.cloned.1.call-done = bf16[40,6144]{1,0:T(8,128)(2,1)} async-done(((bf16[1280,6144]{1,0:T(8,128)(2,1)}), bf16[40,6144]{1,0:T(8,128)(2,1)}) %reduce-scatter.2.cloned.1.call-update) | async-done | bytes 491536 | tf_op jit(solution)/shard_map/reduce_scatter | solution.py:145
  343.4 2.1 convert_element_type.76
  345.4 5.7 %gather_fusion = f32[128,6144]{1,0:T(8,128)} fusion(f32[40,6144]{1,0:T(8,128)} %convert_element_type.76, s32[1024]{0:T(1024)S(1)} %pad_clamp_fusion), kind=kCustom, calls=%fused_computation | custom fusion | bytes 6291968 | tf_op jit(solution)/shard_map/jit(_take)/gather | solution.py:151
  351.1 3.5 fusion.30
  354.6 4.3 %all-to-all-start = ((bf16[4,128,1536]{2,1,0:T(8,128)(2,1)}), bf16[4,128,1536]{2,1,0:T(8,128)(2,1)}, u32[]{:S(2)}, u32[]{:S(2)}) async-start(bf16[4,128,1536]{2,1,0:T(8,128)(2,1)} %fusion.30), calls=%async_computation.1 | async-start | bytes 3145728 | tf_op jit(solution)/shard_map/all_to_all | solution.py:29
  359.0 1.8 constant_dynamic-slice_fusion
  360.7 18.0 %all-to-all-done = bf16[4,128,1536]{2,1,0:T(8,128)(2,1)} async-done(((bf16[4,128,1536]{2,1,0:T(8,128)(2,1)}), bf16[4,128,1536]{2,1,0:T(8,128)(2,1)}, u32[]{:S(2)}, u32[]{:S(2)}) %all-to-all-start) | async-done | bytes 1572896 | tf_op jit(solution)/shard_map/all_to_all | solution.py:29
  378.8 2.5 reduce_sum.31
  (43 shorter events, 2.8 us)
Async XLA Ops:
  7.2 215.9 %copy-start = (bf16[1,256,6144]{2,1,0:T(8,128)(2,1)S(1)}, bf16[1,256,6144]{2,1,0:T(8,128)(2,1)}, u32[]{:S(2)}) copy-start(bf16[1,256,6144]{2,1,0:T(8,128)(2,1)} %param.27) | copy-start | bytes 9437188
  7.2 51.2 %all-gather.5.cloned.1.call-start = ((), (), s32[]{:S(2)}) async-start(), calls=%async_computation.2 | async-start | bytes 2162688 | tf_op jit(solution)/shard_map/all_gather | solution.py:15
  8.8 122.2 %all-reduce.2.cloned.1.call-start = ((), (), s32[]{:S(2)}) async-start(), calls=%async_computation.3 | async-start | bytes 3145728 | tf_op jit(solution)/shard_map/psum | solution.py:122
  11.5 44.2 %copy-start.6 = (s32[128]{0:T(128)}, s32[128]{0:T(128)S(1)}, u32[]{:S(2)}) copy-start(s32[128]{0:T(128)S(1)} %dynamic_slice.10) | copy-start | bytes 1540
  55.8 0.6 copy-start.4
  55.8 0.6 copy-start.7
  61.5 4.0 %copy-start.1 = (pred[128,4096]{1,0:T(8,128)(4,1)S(1)}, pred[128,4096]{1,0:T(8,128)(4,1)}, u32[]{:S(2)}) copy-start(pred[128,4096]{1,0:T(8,128)(4,1)} %compare_and_fusion) | copy-start | bytes 1572868 | tf_op jit(solution)/shard_map/cond
  65.4 4.8 %copy-start.3 = (bf16[4096,256]{1,0:T(8,128)(2,1)S(1)}, bf16[4096,256]{1,0:T(8,128)(2,1)}, u32[]{:S(2)}) copy-start(bf16[4096,256]{1,0:T(8,128)(2,1)} %get-tuple-element.20) | copy-start | bytes 6291460 | tf_op jit(solution)/shard_map/cond
  74.5 6.4 %copy-start.5 = (s32[128,2]{0,1:T(2,128)S(1)}, s32[128,2]{0,1:T(2,128)}, u32[]{:S(2)}) copy-start(s32[128,2]{0,1:T(2,128)} %param.23) | copy-start | bytes 3076
  80.8 53.9 %copy-start.11 = (f32[6144]{0:T(1024)S(1)}, f32[6144]{0:T(1024)}, u32[]{:S(2)}) copy-start(f32[6144]{0:T(1024)} %param.20) | copy-start | bytes 73732
  80.9 125.8 %all-gather.7.cloned.1.call-start = ((), (), s32[]{:S(2)}) async-start(), calls=%async_computation.4 | async-start | bytes 16220160 | tf_op jit(solution)/shard_map/all_gather | solution.py:143
  133.6 1.1 copy-start.2
  136.2 207.2 %reduce-scatter.2.cloned.1.call-start = ((), (), s32[]{:S(2)}) async-start(), calls=%async_computation.5 | async-start | bytes 16220160 | tf_op jit(solution)/shard_map/reduce_scatter | solution.py:145
  206.7 10.8 %copy-start.9 = (bf16[1280,6144]{1,0:T(8,128)(2,1)S(1)}, bf16[1280,6144]{1,0:T(8,128)(2,1)}, u32[]{:S(2)}) copy-start(bf16[1280,6144]{1,0:T(8,128)(2,1)} %all-gather.7.cloned.1.call-done) | copy-start | bytes 47185924
  206.7 11.7 %copy-start.10 = (bf16[1,6144,256]{2,1,0:T(8,128)(2,1)S(1)}, bf16[1,6144,256]{2,1,0:T(8,128)(2,1)}, u32[]{:S(2)}) copy-start(bf16[1,6144,256]{2,1,0:T(8,128)(2,1)} %param.26) | copy-start | bytes 9437188
  230.9 0.7 copy-start.8
  354.6 24.2 %all-to-all-start = ((bf16[4,128,1536]{2,1,0:T(8,128)(2,1)}), bf16[4,128,1536]{2,1,0:T(8,128)(2,1)}, u32[]{:S(2)}, u32[]{:S(2)}) async-start(bf16[4,128,1536]{2,1,0:T(8,128)(2,1)} %fusion.30), calls=%async_computation.1 | async-start | bytes 3145728 | tf_op jit(solution)/shard_map/all_to_all | solution.py:29
Sparse Core Ops, SparseCore 0:
  10.8 46.2 all-gather.4
  81.0 49.9 all-reduce.1
  136.3 70.3 all-gather.6
  231.0 112.3 reduce-scatter.1
where the time goes:
time: 388 us
  waiting for transfers between devices  250 us (64%)
  blocking collectives  43.5 us (11%)
  matrix products  37 us (10%)
  other arithmetic  21.3 us (5%)
  local copies, waits for them, and re-layouts  16.2 us (4%)
  between operations  15.2 us (4%)
  starting transfers between devices  4.68 us (1%)
    reduce_scatter x1, waiting for transfers between devices, local(): lax.psum_scatter(jnp.dot(rows_in, down_weight[0], preferred_element_type=...  112 us
    all_gather x1, waiting for transfers between devices, local(): lax.all_gather(packed, 'cp', axis=0, tiled=True)  70.2 us
    psum x1, waiting for transfers between devices, local(): summed = lax.psum(projected.astype(jnp.bfloat16), 'ep').astype(jnp.float32)  49.7 us
    all_gather x1, blocking collectives, local(): lax.all_gather(own_pos, 'cp', axis=0, tiled=True)  23.1 us
    all_gather x1, blocking collectives, local(): lax.all_gather(own_docs, 'cp', axis=0, tiled=True)  20.4 us
    all_to_all x1, waiting for transfers between devices, summed_on_arrival(): lax.all_to_all(blocks, axis, split_axis=0, concat_axis=0, tiled=True)  18 us
    dot_general x1, matrix products, expert_hidden(): gated = jnp.dot(rows_in, gate_weight[0], preferred_element_type=jnp.float32)  9.37 us
    dot_general x1, matrix products, local(): jnp.dot(rows_in, down_weight[0], preferred_element_type=jnp.float32)  7.79 us
  transfers between devices with their start and end apart: 5, of which 4 were waited for; matrix products, arithmetic and copies ran while one was open for 2% of the time, Pallas kernels for 0%

commit v1 on v0

--- a/solution.py
+++ b/solution.py
@@ -1,13 +1,23 @@
+import functools
 import math
 import jax
 import jax.numpy as jnp
 from jax import lax
 from jax.sharding import PartitionSpec as P
+from jax.lax import all_gather
 
 HD = 128
 CAP = 40
 EPS = 1e-05
 NEG = -1e30
+
+
+def replace_sheet(message, bus_axis):
+    block_out = all_gather(message, bus_axis)
+    return jnp.sum(block_out, axis=0)
+
+
+extend_the_roads = functools.partial(replace_sheet, bus_axis="ep")
 
 
 def in_one_piece(arrays, axis, dim, along):
@@ -119,7 +129,7 @@
     ).astype(jnp.bfloat16)
     projected = jnp.dot(attended, out_weight, preferred_element_type=jnp.float32)
     quarter_width = residual.shape[1] // ep_count
-    summed = lax.psum(projected.astype(jnp.bfloat16), "ep").astype(jnp.float32)
+    summed = extend_the_roads(projected.astype(jnp.bfloat16)).astype(jnp.float32)
     hidden_full = (residual.astype(jnp.float32) + summed).astype(jnp.bfloat16)
     hidden_state = lax.dynamic_slice_in_dim(hidden_full, ep_rank * quarter_width, quarter_width, 1)
     values_wide = hidden_full.astype(jnp.float32)

time: 388 us -> 410 us (1.057)
  waiting for transfers between devices: 250 us -> 266 us
  other arithmetic: 21.3 us -> 26.8 us
    all_gather x0 -> x1, waiting for transfers between devices: none -> 64.7 us  [replace_sheet(): block_out = all_gather(message, bus_axis)]
    psum x1 -> x0, waiting for transfers between devices: 49.7 us -> none  [local(): summed = lax.psum(projected.astype(jnp.bfloat16), 'ep').astype(jnp.float32)]
    reduce_sum x0 -> x1, other arithmetic: none -> 5.53 us  [replace_sheet(): return jnp.sum(block_out, axis=0)]
where the time goes in v1:
time: 410 us; the launch traced here: 409 us
  waiting for transfers between devices  266 us (65%)
  blocking collectives  43.5 us (11%)
  matrix products  37 us (9%)
  other arithmetic  26.8 us (7%)
  local copies, waits for them, and re-layouts  16.2 us (4%)
  between operations  15.2 us (4%)
  starting transfers between devices  4.68 us (1%)
    reduce_scatter x1, waiting for transfers between devices, local(): lax.psum_scatter(jnp.dot(rows_in, down_weight[0], preferred_element_type=...  112 us
    all_gather x1, waiting for transfers between devices, local(): lax.all_gather(packed, 'cp', axis=0, tiled=True)  71.1 us
    all_gather x1, waiting for transfers between devices, replace_sheet(): block_out = all_gather(message, bus_axis)  64.7 us
    all_gather x1, blocking collectives, local(): lax.all_gather(own_pos, 'cp', axis=0, tiled=True)  23.1 us
    all_gather x1, blocking collectives, local(): lax.all_gather(own_docs, 'cp', axis=0, tiled=True)  20.4 us
    all_to_all x1, waiting for transfers between devices, summed_on_arrival(): lax.all_to_all(blocks, axis, split_axis=0, concat_axis=0, tiled=True)  18 us
    dot_general x1, matrix products, expert_hidden(): gated = jnp.dot(rows_in, gate_weight[0], preferred_element_type=jnp.float32)  9.37 us
  transfers between devices with their start and end apart: 5, of which 4 were waited for; matrix products, arithmetic and copies ran while one was open for 2% of the time, Pallas kernels for 0%

profile of v1, /device:TPU:0, one launch (start us, length us, event | category | flops | bytes accessed | tf_op | source)
XLA Modules:
  0.0 409.2 jit_solution(3724546682244724444)
XLA Ops:
  7.2 1.6 pad_maximum_fusion
  8.9 1.2 dynamic_slice.9
  10.8 0.8 dynamic_slice.10
  11.5 23.1 %all-gather.2 = s32[32,1,128]{2,1,0:T(1,128)S(1)} all-gather(s32[1,1,128]{2,1,0:T(1,128)S(1)} %fusion.40), channel_id=1, replica_groups=mesh['cp'=32,'ep'=4] {'cp'}, dimensions={0}, use_global_device_ids=true | all-gather | bytes 16896 | tf_op jit(solution)/shard_map/all_gather | solution.py:114
  35.4 20.4 %all-gather.1 = s32[32,1,128]{2,1,0:T(1,128)S(1)} all-gather(s32[1,1,128]{2,1,0:T(1,128)S(1)} %dynamic-slice_bitcast_fusion), channel_id=1, replica_groups=mesh['cp'=32,'ep'=4] {'cp'}, dimensions={0}, use_global_device_ids=true | all-gather | bytes 16896 | tf_op jit(solution)/shard_map/all_gather | solution.py:113
  56.4 1.3 and_reduce_fusion
  58.4 15.5 %conditional.1 = (f32[128,6]{0,1:T(8,128)}, f32[128,6,128]{0,2,1:T(8,128)S(1)}) conditional(s32[]{:T(128)} %convert_element_type.66, () %tuple.16, (s32[4096]{0:T(1024)}, s32[128]{0:T(128)}, s32[4096]{0:T(1024)S(1)}, s32[128]{0:T(128)}, bf16[128,768]{1,0:T(8,128)(2,1)}, /*index=5*/bf16[4096,256]{1,0:T(8,128)(2,1)}) %tuple.42), branch_computations={%region_1.0_spmd, %region_2.5_spmd} | conditional | flops 1653079296 | bytes 53465160 | solution.py:120
  58.4 2.0 compare_and_fusion
  60.4 1.1 copy.79
  61.5 3.9 fusion
  65.5 4.7 %fusion.2 = f32[128,6]{0,1:T(8,128)} fusion(f32[128,6,4096]{2,0,1:T(8,128)S(1)} %get-tuple-element.61, f32[128,6]{0,1:T(8,128)S(1)} %broadcast_maximum_fusion, pred[128,4096]{1,0:T(8,128)(4,1)S(1)} %copy-done.1), kind=kLoop, calls=%fused_computation.5 | loop fusion | flops 15727872 | bytes 13113344 | tf_op jit(solution)/shard_map/cond/branch_1_fun/reduce_sum | solution.py:91
  70.2 3.6 fusion.3
  74.6 6.3 %convolution_convert_fusion.1 = bf16[128,6144]{1,0:T(8,128)(2,1)} fusion(bf16[128,768]{0,1:T(8,128)(2,1)S(1)} %bitcast.59, bf16[768,6144]{1,0:T(8,128)(2,1)} %param.19), kind=kOutput, calls=%fused_computation.19 | convolution fusion | flops 1208745984 | bytes 11206656 | tf_op jit(solution)/shard_map/dot_general | solution.py:130
  81.5 64.7 %all-gather.11.cloned.1.call-done = bf16[512,6144]{1,0:T(8,128)(2,1)} async-done(((bf16[128,6144]{1,0:T(8,128)(2,1)}), bf16[512,6144]{1,0:T(8,128)(2,1)}) %all-gather.11.cloned.1.call-update) | async-done | bytes 6291472 | tf_op jit(solution)/shard_map/all_gather | solution.py:16
  146.2 5.5 %reduce_sum.42 = bf16[128,6144]{1,0:T(8,128)(2,1)} reduce(bf16[4,128,6144]{2,1,0:T(8,128)(2,1)} %bitcast.58, bf16[]{:T(256)} %constant.37.clone.1), dimensions={0}, to_apply=%region_5.6 | reduce | flops 2359296 | bytes 7864322 | tf_op jit(solution)/shard_map/reduce_sum | solution.py:17
  151.7 2.6 fusion.14
  154.4 1.1 copy-done.2
  155.5 1.4 convolution_convert_fusion.2
  157.0 71.1 %all-gather.9.cloned.1.call-done = bf16[1280,6144]{1,0:T(8,128)(2,1)} async-done(((bf16[40,6144]{1,0:T(8,128)(2,1)}), bf16[1280,6144]{1,0:T(8,128)(2,1)}) %all-gather.9.cloned.1.call-update) | async-done | bytes 15728656 | tf_op jit(solution)/shard_map/all_gather | solution.py:153
  228.1 9.4 %fusion.22 = f32[1280,256]{1,0:T(8,128)S(1)} fusion(bf16[1280,6144]{1,0:T(8,128)(2,1)} %all-gather.9.cloned.1.call-done, bf16[1,6144,256]{2,1,0:T(8,128)(2,1)} %param.25), kind=kOutput, calls=%fused_computation.32 | convolution fusion | flops 4026531840 | bytes 20185088 | tf_op jit(solution)/shard_map/dot_general | solution.py:44
  237.5 1.5 copy-done.9
  238.9 0.9 copy-done.10
  239.8 4.6 %fusion.27 = bf16[1280,256]{1,0:T(8,128)(2,1)S(1)} fusion(bf16[1280,6144]{1,0:T(8,128)(2,1)S(1)} %copy-done.9, bf16[1,6144,256]{2,1,0:T(8,128)(2,1)S(1)} %copy-done.10, f32[1280,256]{1,0:T(8,128)S(1)} %fusion.22), kind=kOutput, calls=%fused_computation.36 | convolution fusion | flops 4028497920 | bytes 20840448 | tf_op jit(solution)/shard_map/dot_general | solution.py:45
  244.4 7.8 %convolution_convert_fusion = bf16[1280,6144]{1,0:T(8,128)(2,1)} fusion(bf16[1280,256]{1,0:T(8,128)(2,1)S(1)} %fusion.27, bf16[1,256,6144]{2,1,0:T(8,128)(2,1)S(1)} %copy-done), kind=kOutput, calls=%fused_computation.18 | convolution fusion | flops 4034396160 | bytes 19529728 | tf_op jit(solution)/shard_map/dot_general | solution.py:156
  252.9 111.8 %reduce-scatter.2.cloned.1.call-done = bf16[40,6144]{1,0:T(8,128)(2,1)} async-done(((bf16[1280,6144]{1,0:T(8,128)(2,1)}), bf16[40,6144]{1,0:T(8,128)(2,1)}) %reduce-scatter.2.cloned.1.call-update) | async-done | bytes 491536 | tf_op jit(solution)/shard_map/reduce_scatter | solution.py:155
  364.8 2.1 convert_element_type.78
  366.8 5.7 %gather_fusion = f32[128,6144]{1,0:T(8,128)} fusion(f32[40,6144]{1,0:T(8,128)} %convert_element_type.78, s32[1024]{0:T(1024)S(1)} %pad_clamp_fusion), kind=kCustom, calls=%fused_computation | custom fusion | bytes 6291968 | tf_op jit(solution)/shard_map/jit(_take)/gather | solution.py:161
  372.5 3.5 fusion.30
  376.0 4.3 %all-to-all-start = ((bf16[4,128,1536]{2,1,0:T(8,128)(2,1)}), bf16[4,128,1536]{2,1,0:T(8,128)(2,1)}, u32[]{:S(2)}, u32[]{:S(2)}) async-start(bf16[4,128,1536]{2,1,0:T(8,128)(2,1)} %fusion.30), calls=%async_computation.1 | async-start | bytes 3145728 | tf_op jit(solution)/shard_map/all_to_all | solution.py:39
  380.4 1.8 constant_dynamic-slice_fusion
  382.1 18.0 %all-to-all-done = bf16[4,128,1536]{2,1,0:T(8,128)(2,1)} async-done(((bf16[4,128,1536]{2,1,0:T(8,128)(2,1)}), bf16[4,128,1536]{2,1,0:T(8,128)(2,1)}, u32[]{:S(2)}, u32[]{:S(2)}) %all-to-all-start) | async-done | bytes 1572896 | tf_op jit(solution)/shard_map/all_to_all | solution.py:39
  400.2 2.5 reduce_sum.44
  (44 shorter events, 3.6 us)
Async XLA Ops:
  7.2 237.3 %copy-start = (bf16[1,256,6144]{2,1,0:T(8,128)(2,1)S(1)}, bf16[1,256,6144]{2,1,0:T(8,128)(2,1)}, u32[]{:S(2)}) copy-start(bf16[1,256,6144]{2,1,0:T(8,128)(2,1)} %param.27) | copy-start | bytes 9437188
  7.2 51.2 %all-gather.7.cloned.1.call-start = ((), (), s32[]{:S(2)}) async-start(), calls=%async_computation.2 | async-start | bytes 2162688 | tf_op jit(solution)/shard_map/all_gather | solution.py:25
  8.8 137.3 %all-gather.11.cloned.1.call-start = ((), (), s32[]{:S(2)}) async-start(), calls=%async_computation.5 | async-start | bytes 7864320 | tf_op jit(solution)/shard_map/all_gather | solution.py:16
  11.5 44.2 %copy-start.6 = (s32[128]{0:T(128)}, s32[128]{0:T(128)S(1)}, u32[]{:S(2)}) copy-start(s32[128]{0:T(128)S(1)} %dynamic_slice.10) | copy-start | bytes 1540
  55.8 0.6 copy-start.4
  55.8 0.6 copy-start.7
  61.5 4.0 copy-start.1
  65.4 4.8 %copy-start.3 = (bf16[4096,256]{1,0:T(8,128)(2,1)S(1)}, bf16[4096,256]{1,0:T(8,128)(2,1)}, u32[]{:S(2)}) copy-start(bf16[4096,256]{1,0:T(8,128)(2,1)} %get-tuple-element.20) | copy-start | bytes 6291460 | tf_op jit(solution)/shard_map/cond
  74.5 6.5 %copy-start.5 = (s32[128,2]{0,1:T(2,128)S(1)}, s32[128,2]{0,1:T(2,128)}, u32[]{:S(2)}) copy-start(s32[128,2]{0,1:T(2,128)} %param.23) | copy-start | bytes 3076
  80.9 147.2 %all-gather.9.cloned.1.call-start = ((), (), s32[]{:S(2)}) async-start(), calls=%async_computation.3 | async-start | bytes 16220160 | tf_op jit(solution)/shard_map/all_gather | solution.py:153
  151.7 3.8 copy-start.11
  154.3 1.1 copy-start.2
  156.9 207.8 %reduce-scatter.2.cloned.1.call-start = ((), (), s32[]{:S(2)}) async-start(), calls=%async_computation.4 | async-start | bytes 16220160 | tf_op jit(solution)/shard_map/reduce_scatter | solution.py:155
  228.1 10.8 %copy-start.9 = (bf16[1280,6144]{1,0:T(8,128)(2,1)S(1)}, bf16[1280,6144]{1,0:T(8,128)(2,1)}, u32[]{:S(2)}) copy-start(bf16[1280,6144]{1,0:T(8,128)(2,1)} %all-gather.9.cloned.1.call-done) | copy-start | bytes 47185924
  228.1 11.7 %copy-start.10 = (bf16[1,6144,256]{2,1,0:T(8,128)(2,1)S(1)}, bf16[1,6144,256]{2,1,0:T(8,128)(2,1)}, u32[]{:S(2)}) copy-start(bf16[1,6144,256]{2,1,0:T(8,128)(2,1)} %param.26) | copy-start | bytes 9437188
  252.2 0.7 copy-start.8
  376.0 24.2 %all-to-all-start = ((bf16[4,128,1536]{2,1,0:T(8,128)(2,1)}), bf16[4,128,1536]{2,1,0:T(8,128)(2,1)}, u32[]{:S(2)}, u32[]{:S(2)}) async-start(bf16[4,128,1536]{2,1,0:T(8,128)(2,1)} %fusion.30), calls=%async_computation.1 | async-start | bytes 3145728 | tf_op jit(solution)/shard_map/all_to_all | solution.py:39
Sparse Core Ops, SparseCore 0:
  10.8 46.2 all-gather.6
  81.0 65.1 all-gather.10
  157.1 70.9 all-gather.8
  252.4 112.3 reduce-scatter.1
